TPU v7x, 32 devices: a whole 2x2x4 slice. The times are simulated.
32 devices in a mesh: blk: 8 (over y, x, core), pix: 4 (over z).
Axes of the slice: x: 2, y: 2, z: 4, core: 2. Of those that a mesh axis runs over, the one named last changes fastest.
Arguments:
- particles: bfloat16 [4096, 16384], P('blk', 'pix'), may hold values from -10 to 10, as said below
- ctf: bfloat16 [4096, 16384], P('blk', 'pix'), may hold values from -1 to 1
- noise_var: float32 [16384], P('pix'), may hold values from 0.5 to 4
- projections: bfloat16 [128, 16384], P('blk', 'pix'), may hold values from -3.1 to 3.1
- orient_class: int32 [128], replicated, may hold values from 0 to 4
- class_prior: float32 [5], replicated, may hold values from -2 to 0
- counts: int32 [8], P('blk'), may hold values from 32 to 512, as said below
Outputs:
- class_field: float32 [128, 16384], P('blk', 'pix')
- normalizer: float32 [4096], P('blk')
Inputs may be any that keep to these rules, and one draw needn't show every extreme that they name: `particles`: real values of particle images. Live slots of each index of blk are its first counts slots; some index of blk is full in every draw.
All inputs are finite; a program needn't handle non-finite values.
Results may differ from a plain program's by a relative error of at most 0.0066.
Values may be sent and summed in bfloat16 or wider, within the bound.
No kernel may reach another device: no remote copies, remote signals or barrier semaphores. Data moves between devices by JAX's collectives and lax.ppermute only.
A program may use at most 128 MiB of HBM per device.

v0:
```python
import jax
import jax.numpy as jnp
from jax import lax
from jax.sharding import PartitionSpec as P

CLASSES = 5


def body(particles, ctf, noise_var, projections, orient_class, class_prior, counts):
    inverse = 1.0 / noise_var
    ctf_wide = ctf.astype(jnp.float32)
    weighted = (particles.astype(jnp.float32) * ctf_wide * inverse[None, :]).astype(jnp.bfloat16)
    quadratic = (0.5 * ctf_wide * ctf_wide * inverse[None, :]).astype(jnp.bfloat16)
    member = orient_class[:, None] == jnp.arange(CLASSES, dtype=jnp.int32)[None, :]
    orient_prior = jnp.sum(jnp.where(member, class_prior[None, :], jnp.float32(0.0)), axis=1)
    slot_count = particles.shape[0]
    live_slot = jnp.arange(slot_count, dtype=jnp.int32) < counts[0]
    part_rows = lax.all_gather(projections, "blk", axis=0, tiled=True)
    rows_wide = part_rows.astype(jnp.float32)
    piece_square = (rows_wide * rows_wide).astype(jnp.bfloat16)
    cross_term = lax.dot_general(
        weighted, part_rows, (((1,), (1,)), ((), ())), preferred_element_type=jnp.float32
    )
    square_term = lax.dot_general(
        quadratic, piece_square, (((1,), (1,)), ((), ())), preferred_element_type=jnp.float32
    )
    partial_value = cross_term - square_term
    scores = lax.psum(partial_value, "pix")
    logits = scores + orient_prior[None, :]
    peak_score = jnp.max(logits, axis=1)
    log_total = peak_score + jnp.log(jnp.sum(jnp.exp(logits - peak_score[:, None]), axis=1))
    weights = jnp.where(
        live_slot[:, None], jnp.exp(logits - log_total[:, None]), jnp.float32(0.0)
    ).astype(jnp.bfloat16)
    normalizer = jnp.where(live_slot, log_total, jnp.float32(0.0))
    class_field = lax.psum_scatter(
        lax.dot_general(
            weights, weighted, (((0,), (0,)), ((), ())), preferred_element_type=jnp.float32
        ),
        "blk",
        scatter_dimension=0,
        tiled=True,
    )
    return (class_field, normalizer)


def solution(mesh):
    placed = (P("blk", "pix"), P("blk", "pix"), P("pix"), P("blk", "pix"), P(), P(), P("blk"))
    return jax.shard_map(
        body, mesh=mesh, in_specs=placed, out_specs=(P("blk", "pix"), P("blk")), check_vma=False
    )
```

profile of v0, /device:TPU:0, one launch (start us, length us, event | category | flops | bytes accessed | tf_op | source)
XLA Modules:
  0.0 136.5 jit_solution(207388093843706414)
XLA Ops:
  7.2 0.0 all-gather.2.cloned.1.call-start
  7.2 0.7 all-gather.2.cloned.1.call-update
  7.9 0.0 all-reduce.2.cloned.1.call-start
  7.9 0.7 broadcast_divide_fusion
  8.7 27.3 %all-gather.2.cloned.1.call-done = bf16[128,4096]{1,0:T(8,128)(2,1)} async-done(((bf16[16,4096]{1,0:T(8,128)(2,1)}), bf16[128,4096]{1,0:T(8,128)(2,1)}) %all-gather.2.cloned.1.call-update) | async-done | bytes 1048592 | tf_op jit(solution)/shard_map/all_gather | solution.py:18
  36.0 0.0 copy-start
  36.0 0.0 copy-start.1
  36.0 5.3 %fusion.11 = f32[512,128]{1,0:T(8,128)S(1)} fusion(bf16[128,4096]{1,0:T(8,128)(2,1)} %all-gather.2.cloned.1.call-done, bf16[512,4096]{1,0:T(8,128)(2,1)} %param.8, bf16[512,4096]{1,0:T(8,128)(2,1)} %param.7, f32[4096]{0:T(1024)S(1)} %broadcast_divide_fusion), kind=kOutput, calls=%fused_computation.10 | convolution fusion | flops 547356672 | bytes 9715712 | tf_op jit(solution)/shard_map/dot_general | solution.py:21
  41.3 0.0 copy-done
  41.3 0.0 copy-done.1
  41.3 0.0 copy-start.2
  41.3 0.0 copy-start.3
  41.3 2.2 %fusion.6 = f32[512,128]{1,0:T(8,128)} fusion(f32[512,128]{1,0:T(8,128)S(1)} %fusion.11, bf16[512,4096]{1,0:T(8,128)(2,1)S(1)} %copy-done, f32[4096]{0:T(1024)S(1)} %broadcast_divide_fusion, bf16[128,4096]{1,0:T(8,128)(2,1)S(1)} %copy-done.1), kind=kOutput, calls=%fused_computation.8 | convolution fusion | flops 548995072 | bytes 5783552 | tf_op jit(solution)/shard_map/dot_general | solution.py:24
  43.5 0.0 all-reduce.2.cloned.1.call-update
  43.6 0.0 reduce-scatter.2.cloned.1.call-start
  44.3 0.0 copy-done.2
  44.3 0.0 copy-done.3
  44.3 0.1 select_reduce_fusion
  44.4 34.9 %all-reduce.2.cloned.1.call-done = f32[512,128]{1,0:T(8,128)} async-done(((f32[512,128]{1,0:T(8,128)}), f32[512,128]{1,0:T(8,128)}) %all-reduce.2.cloned.1.call-update) | async-done | bytes 262160 | tf_op jit(solution)/shard_map/psum | solution.py:28
  79.3 1.1 add_reduce_fusion
  80.4 1.2 exponential_reduce_fusion
  81.6 0.6 broadcast_select_fusion
  82.2 6.7 %fusion.9 = f32[128,4096]{1,0:T(8,128)} fusion(bf16[512,4096]{1,0:T(8,128)(2,1)} %param.8, bf16[512,4096]{1,0:T(8,128)(2,1)} %param.7, f32[4096]{0:T(1024)S(1)} %broadcast_divide_fusion, f32[512,128]{1,0:T(8,128)} %all-reduce.2.cloned.1.call-done, f32[512]{0:T(512)S(1)} %get-tuple-element.3, f32[128]{0:T(128)S(1)} %select_reduce_fusion, ...), kind=kOutput, calls=%fused_computation.9 | convolution fusion | flops 547618816 | bytes 10767360 | tf_op jit(solution)/shard_map/dot_general | solution.py:37
  88.9 0.0 reduce-scatter.2.cloned.1.call-update
  88.9 41.1 %reduce-scatter.2.cloned.1.call-done = f32[16,4096]{1,0:T(8,128)} async-done(((f32[128,4096]{1,0:T(8,128)}), f32[16,4096]{1,0:T(8,128)}) %reduce-scatter.2.cloned.1.call-update) | async-done | bytes 262160 | tf_op jit(solution)/shard_map/reduce_scatter | solution.py:36
  (1 shorter events, 0.0 us)
Async XLA Ops:
  7.2 28.8 %all-gather.2.cloned.1.call-start = ((), (), s32[]{:S(2)}) async-start(), calls=%async_computation.1 | async-start | bytes 1179648 | tf_op jit(solution)/shard_map/all_gather | solution.py:18
  7.9 71.4 %all-reduce.2.cloned.1.call-start = ((), (), s32[]{:S(2)}) async-start(), calls=%async_computation.2 | async-start | bytes 524288 | tf_op jit(solution)/shard_map/psum | solution.py:28
  36.0 5.3 %copy-start = (bf16[512,4096]{1,0:T(8,128)(2,1)S(1)}, bf16[512,4096]{1,0:T(8,128)(2,1)}, u32[]{:S(2)}) copy-start(bf16[512,4096]{1,0:T(8,128)(2,1)} %param.8) | copy-start | bytes 12582916
  36.0 5.3 %copy-start.1 = (bf16[128,4096]{1,0:T(8,128)(2,1)S(1)}, bf16[128,4096]{1,0:T(8,128)(2,1)}, u32[]{:S(2)}) copy-start(bf16[128,4096]{1,0:T(8,128)(2,1)} %all-gather.2.cloned.1.call-done) | copy-start | bytes 3145732
  41.3 3.0 %copy-start.2 = (f32[5]{0:T(128)S(1)}, f32[5]{0:T(128)}, u32[]{:S(2)}) copy-start(f32[5]{0:T(128)} %param.12) | copy-start | bytes 64
  41.3 3.0 %copy-start.3 = (s32[128]{0:T(128)S(1)}, s32[128]{0:T(128)}, u32[]{:S(2)}) copy-start(s32[128]{0:T(128)} %param.11) | copy-start | bytes 1540
  43.6 86.4 %reduce-scatter.2.cloned.1.call-start = ((), (), s32[]{:S(2)}) async-start(), calls=%async_computation.3 | async-start | bytes 2359296 | tf_op jit(solution)/shard_map/reduce_scatter | solution.py:36
Sparse Core Ops, SparseCore 0:
  9.9 26.0 all-gather.1
  43.7 35.5 all-reduce.1
  89.0 40.9 reduce-scatter.1
where the time goes:
time: 137 us
  waiting for transfers between devices  104 us (76%)
  between operations  14.5 us (11%)
  matrix products  14.2 us (10%)
  other arithmetic  3.69 us (3%)
    reduce_scatter x1, waiting for transfers between devices, body(): lax.psum_scatter(lax.dot_general(weights, weighted, (((0,), (0,)), ((), (...  41.1 us
    psum x1, waiting for transfers between devices, body(): scores = lax.psum(partial_value, 'pix')  34.9 us
    all_gather x1, waiting for transfers between devices, body(): part_rows = lax.all_gather(projections, 'blk', axis=0, tiled=True)  27.3 us
    dot_general x1, matrix products, body(): lax.dot_general(weights, weighted, (((0,), (0,)), ((), ())), preferred_el...  6.68 us
    dot_general x1, matrix products, body(): lax.dot_general(weighted, part_rows, (((1,), (1,)), ((), ())), preferred_...  5.26 us
  transfers between devices with their start and end apart: 3, of which 3 were waited for; matrix products, arithmetic and copies ran while one was open for 1% of the time, Pallas kernels for 0%

commit v1 on v0

--- a/solution.py
+++ b/solution.py
@@ -25,7 +25,7 @@
         quadratic, piece_square, (((1,), (1,)), ((), ())), preferred_element_type=jnp.float32
     )
     partial_value = cross_term - square_term
-    scores = lax.psum(partial_value, "pix")
+    scores = jnp.sum(lax.all_gather(partial_value, "pix"), axis=0)
     logits = scores + orient_prior[None, :]
     peak_score = jnp.max(logits, axis=1)
     log_total = peak_score + jnp.log(jnp.sum(jnp.exp(logits - peak_score[:, None]), axis=1))

time: 137 us -> 128 us (0.934)
  waiting for transfers between devices: 104 us -> 96 us
    psum x1 -> x0, waiting for transfers between devices: 34.9 us -> none  [body(): scores = lax.psum(partial_value, 'pix')]
    all_gather x0 -> x1, waiting for transfers between devices: none -> 27.3 us  [body(): scores = jnp.sum(lax.all_gather(partial_value, 'pix'), axis=0)]
where the time goes in v1:
time: 128 us
  waiting for transfers between devices  96 us (75%)
  between operations  14.5 us (11%)
  matrix products  14.1 us (11%)
  other arithmetic  3.11 us (2%)
    reduce_scatter x1, waiting for transfers between devices, body(): lax.psum_scatter(lax.dot_general(weights, weighted, (((0,), (0,)), ((), (...  40.7 us
    all_gather x1, waiting for transfers between devices, body(): scores = jnp.sum(lax.all_gather(partial_value, 'pix'), axis=0)  27.3 us
    all_gather x1, waiting for transfers between devices, body(): part_rows = lax.all_gather(projections, 'blk', axis=0, tiled=True)  27.3 us
    dot_general x1, matrix products, body(): lax.dot_general(weights, weighted, (((0,), (0,)), ((), ())), preferred_el...  6.61 us
    dot_general x1, matrix products, body(): lax.dot_general(weighted, part_rows, (((1,), (1,)), ((), ())), preferred_...  5.26 us
  transfers between devices with their start and end apart: 3, of which 3 were waited for; matrix products, arithmetic and copies ran while one was open for 1% of the time, Pallas kernels for 0%

profile of v1, /device:TPU:0, one launch (start us, length us, event | category | flops | bytes accessed | tf_op | source)
XLA Modules:
  0.0 127.8 jit_solution(2215945341152516730)
XLA Ops:
  7.2 0.0 all-gather.4.cloned.1.call-start
  7.2 0.7 all-gather.4.cloned.1.call-update
  7.9 0.0 all-gather.6.cloned.1.call-start
  7.9 0.7 broadcast_divide_fusion
  8.7 27.3 %all-gather.4.cloned.1.call-done = bf16[128,4096]{1,0:T(8,128)(2,1)} async-done(((bf16[16,4096]{1,0:T(8,128)(2,1)}), bf16[128,4096]{1,0:T(8,128)(2,1)}) %all-gather.4.cloned.1.call-update) | async-done | bytes 1048592 | tf_op jit(solution)/shard_map/all_gather | solution.py:18
  36.0 0.0 copy-start
  36.0 0.0 copy-start.1
  36.0 5.3 %fusion.11 = f32[512,128]{1,0:T(8,128)S(1)} fusion(bf16[128,4096]{1,0:T(8,128)(2,1)} %all-gather.4.cloned.1.call-done, bf16[512,4096]{1,0:T(8,128)(2,1)} %param.8, bf16[512,4096]{1,0:T(8,128)(2,1)} %param.7, f32[4096]{0:T(1024)S(1)} %broadcast_divide_fusion), kind=kOutput, calls=%fused_computation.10 | convolution fusion | flops 547356672 | bytes 9715712 | tf_op jit(solution)/shard_map/dot_general | solution.py:21
  41.3 0.0 copy-done
  41.3 0.0 copy-done.1
  41.3 0.0 copy-start.2
  41.3 0.0 copy-start.3
  41.3 2.2 %fusion.6 = f32[512,128]{1,0:T(8,128)} fusion(f32[512,128]{1,0:T(8,128)S(1)} %fusion.11, bf16[512,4096]{1,0:T(8,128)(2,1)S(1)} %copy-done, f32[4096]{0:T(1024)S(1)} %broadcast_divide_fusion, bf16[128,4096]{1,0:T(8,128)(2,1)S(1)} %copy-done.1), kind=kOutput, calls=%fused_computation.8 | convolution fusion | flops 548995072 | bytes 5783552 | tf_op jit(solution)/shard_map/dot_general | solution.py:24
  43.5 0.0 all-gather.6.cloned.1.call-update
  43.6 0.0 reduce-scatter.2.cloned.1.call-start
  44.3 0.0 copy-done.2
  44.3 0.0 copy-done.3
  44.3 0.1 select_reduce_fusion
  44.4 27.3 %all-gather.6.cloned.1.call-done = f32[2048,128]{1,0:T(8,128)} async-done(((f32[512,128]{1,0:T(8,128)}), f32[2048,128]{1,0:T(8,128)}) %all-gather.6.cloned.1.call-update) | async-done | bytes 1048592 | tf_op jit(solution)/shard_map/all_gather | solution.py:28
  71.7 1.3 %reduce_sum.27 = f32[512,128]{1,0:T(8,128)S(1)} reduce(f32[4,512,128]{2,1,0:T(8,128)} %bitcast.5, f32[]{:T(128)} %constant.2.clone.1), dimensions={0}, to_apply=%region_0.1 | reduce | flops 196608 | bytes 1310724 | tf_op jit(solution)/shard_map/reduce_sum | solution.py:28
  73.0 0.1 add_reduce_fusion
  73.2 0.2 exponential_reduce_fusion
  73.4 0.6 broadcast_select_fusion
  74.0 6.6 %fusion.9 = f32[128,4096]{1,0:T(8,128)} fusion(bf16[512,4096]{1,0:T(8,128)(2,1)} %param.8, bf16[512,4096]{1,0:T(8,128)(2,1)} %param.7, f32[4096]{0:T(1024)S(1)} %broadcast_divide_fusion, f32[512,128]{1,0:T(8,128)S(1)} %reduce_sum.27, f32[512]{0:T(512)S(1)} %get-tuple-element.3, f32[128]{0:T(128)S(1)} %select_reduce_fusion, ...), kind=kOutput, calls=%fused_computation.9 | convolution fusion | flops 547618816 | bytes 10767360 | tf_op jit(solution)/shard_map/dot_general | solution.py:37
  80.6 0.0 reduce-scatter.2.cloned.1.call-update
  80.6 40.7 %reduce-scatter.2.cloned.1.call-done = f32[16,4096]{1,0:T(8,128)} async-done(((f32[128,4096]{1,0:T(8,128)}), f32[16,4096]{1,0:T(8,128)}) %reduce-scatter.2.cloned.1.call-update) | async-done | bytes 262160 | tf_op jit(solution)/shard_map/reduce_scatter | solution.py:36
  (1 shorter events, 0.0 us)
Async XLA Ops:
  7.2 28.8 %all-gather.4.cloned.1.call-start = ((), (), s32[]{:S(2)}) async-start(), calls=%async_computation.1 | async-start | bytes 1179648 | tf_op jit(solution)/shard_map/all_gather | solution.py:18
  7.9 63.8 %all-gather.6.cloned.1.call-start = ((), (), s32[]{:S(2)}) async-start(), calls=%async_computation.3 | async-start | bytes 1310720 | tf_op jit(solution)/shard_map/all_gather | solution.py:28
  36.0 5.3 %copy-start = (bf16[512,4096]{1,0:T(8,128)(2,1)S(1)}, bf16[512,4096]{1,0:T(8,128)(2,1)}, u32[]{:S(2)}) copy-start(bf16[512,4096]{1,0:T(8,128)(2,1)} %param.8) | copy-start | bytes 12582916
  36.0 5.3 %copy-start.1 = (bf16[128,4096]{1,0:T(8,128)(2,1)S(1)}, bf16[128,4096]{1,0:T(8,128)(2,1)}, u32[]{:S(2)}) copy-start(bf16[128,4096]{1,0:T(8,128)(2,1)} %all-gather.4.cloned.1.call-done) | copy-start | bytes 3145732
  41.3 3.0 %copy-start.2 = (f32[5]{0:T(128)S(1)}, f32[5]{0:T(128)}, u32[]{:S(2)}) copy-start(f32[5]{0:T(128)} %param.12) | copy-start | bytes 64
  41.3 3.0 %copy-start.3 = (s32[128]{0:T(128)S(1)}, s32[128]{0:T(128)}, u32[]{:S(2)}) copy-start(s32[128]{0:T(128)} %param.11) | copy-start | bytes 1540
  43.6 77.7 %reduce-scatter.2.cloned.1.call-start = ((), (), s32[]{:S(2)}) async-start(), calls=%async_computation.2 | async-start | bytes 2359296 | tf_op jit(solution)/shard_map/reduce_scatter | solution.py:36
Sparse Core Ops, SparseCore 0:
  9.9 26.0 all-gather.3
  43.7 27.9 all-gather.5
  80.7 40.4 reduce-scatter.1
